TPU v7x, 32 devices: a whole 2x2x4 slice. The times are simulated.
32 devices in a mesh: groups: 2 (over x), blk: 8 (over z, y), rep: 2 (over core).
Axes of the slice: x: 2, y: 2, z: 4, core: 2. Of those that a mesh axis runs over, the one named last changes fastest.
Arguments:
- resident: bfloat16 [32768, 768], P(('groups', 'blk', 'rep')), parts along dimension 0, may hold values from -600 to 600
- ingest: bfloat16 [16384, 768], P(('groups', 'blk', 'rep')), parts along dimension 0, may hold values from -600 to 600
- cluster_ids: int32 [16384], P(('groups', 'blk', 'rep')), parts along dimension 0, may hold values from 0 to 127, as said below
Outputs:
- resident_score: float32 [32768], P(('groups', 'blk', 'rep')), parts along dimension 0
- ingest_score: float32 [16384], P(('groups', 'blk', 'rep')), parts along dimension 0
There are 2 independent parts, one for each index of `groups`. A program takes and returns all parts, laid end to end along the dimension named above; each array names one. Nothing has to cross between parts.
Inputs may be any that keep to these rules, and one draw needn't show every extreme that they name: `cluster_ids`: clusters 16 * p to 16 * p + 15 belong to cycle position p. At most 96 documents of one device belong to one cycle position, and in every draw some cycle position receives 96 from every device.
All inputs are finite; a program needn't handle non-finite values.
Results may differ from a plain program's by a relative error of at most 0.0003.
Values may be sent and summed in bfloat16 or wider, within the bound.
A program may use at most 64 MiB of HBM per device.

v0:
```python
import jax
import jax.numpy as jnp
from jax import lax
from jax.sharding import PartitionSpec as P

INGEST_DEV = 512
CL_OWN = 16
CYCLE_STEPS = 4


temper = 0.2
epsilon = 1e-06


def shifted(value, axis, steps):
    count = lax.axis_size(axis)
    pairs = [(source, (source + steps) % count) for source in range(count)]
    return lax.ppermute(value, axis, pairs)


def unit_rows(rows):
    values = rows.astype(jnp.float32)
    squares = jnp.sum(values * values, axis=-1, keepdims=True) + epsilon
    factor = lax.rsqrt(squares)
    return (values * factor).astype(jnp.bfloat16)


def kernel_sums(visitors, occupancy, residents):
    count_rows = visitors.shape[0]
    block_rows = 512
    num_blocks = count_rows // block_rows
    visit_blocks = visitors.reshape(num_blocks, block_rows, visitors.shape[1])
    live_blocks = occupancy.astype(jnp.float32).reshape(num_blocks, block_rows)

    def tile_sums(running, pieces):
        visit_tile, live_tile = pieces
        scores = jnp.einsum("vd,rd->vr", visit_tile, residents, preferred_element_type=jnp.float32)
        kernel = jnp.exp((scores - 1.0) / temper)
        return (running + jnp.sum(kernel * live_tile[:, None], axis=0), jnp.sum(kernel, axis=1))

    resident_part, visit_parts = lax.scan(
        tile_sums, jnp.zeros((residents.shape[0],), jnp.float32), (visit_blocks, live_blocks)
    )
    return (visit_parts.reshape(count_rows), resident_part)


def on_device(resident, ingest, cluster_ids):
    cycle_size = lax.axis_size("blk")
    slot_count = 3 * INGEST_DEV // (2 * cycle_size)
    columns = ingest.shape[1]
    owners = cluster_ids // CL_OWN
    onehot = (owners[:, None] == jnp.arange(cycle_size, dtype=jnp.int32)[None, :]).astype(jnp.int32)
    rank_within = jnp.sum((jnp.cumsum(onehot, axis=0) - onehot) * onehot, axis=1)
    targets = owners * slot_count + rank_within
    unit_ingest = unit_rows(ingest)
    outgoing = (
        jnp.zeros((cycle_size * slot_count, columns), jnp.bfloat16).at[targets].set(unit_ingest)
    )
    filled = (
        jnp.zeros((cycle_size * slot_count,), jnp.bfloat16)
        .at[targets]
        .set(jnp.ones((ingest.shape[0],), jnp.bfloat16))
    )
    arrived, present = (
        lax.all_to_all(
            outgoing.reshape(cycle_size, slot_count, columns),
            "blk",
            split_axis=0,
            concat_axis=0,
            tiled=True,
        ),
        lax.all_to_all(
            filled.reshape(cycle_size, slot_count), "blk", split_axis=0, concat_axis=0, tiled=True
        ),
    )
    visitors, marked = (
        lax.all_gather(
            arrived.reshape(cycle_size * slot_count, columns), "rep", axis=0, tiled=True
        ),
        lax.all_gather(present.reshape(cycle_size * slot_count), "rep", axis=0, tiled=True),
    )
    unit_resident = unit_rows(resident)
    visit_total = jnp.zeros((visitors.shape[0],), jnp.float32)
    resident_total = jnp.zeros((resident.shape[0],), jnp.float32)
    moving = unit_resident
    for rotation in range(CYCLE_STEPS + 1):
        if rotation > 0:
            moving = shifted(moving, "blk", -1)
            resident_total = shifted(resident_total, "blk", -1)
        visit_part, resident_part = kernel_sums(visitors, marked, moving)
        visit_total = visit_total + visit_part
        resident_total = resident_total + resident_part
    resident_total = shifted(resident_total, "blk", CYCLE_STEPS)
    own_sums = lax.psum_scatter(visit_total, "rep", scatter_dimension=0, tiled=True)
    returned = lax.all_to_all(
        own_sums.reshape(cycle_size, slot_count), "blk", split_axis=0, concat_axis=0, tiled=True
    )
    density = returned.reshape(cycle_size * slot_count)[targets]
    return (jnp.log1p(resident_total), jnp.log1p(density))


def solution(mesh):
    in_specs = (
        P(("groups", "blk", "rep"), None),
        P(("groups", "blk", "rep"), None),
        P(("groups", "blk", "rep")),
    )
    out_specs = (P(("groups", "blk", "rep")), P(("groups", "blk", "rep")))
    return jax.shard_map(
        on_device, mesh=mesh, in_specs=in_specs, out_specs=out_specs, check_vma=False
    )
```

profile of v0, /device:TPU:0, one launch (start us, length us, event | category | flops | bytes accessed | tf_op | source)
XLA Modules:
  0.0 246.6 jit_solution(1169639654223723003)
XLA Ops:
  7.2 0.7 fusion.45
  7.9 0.7 add_select_fusion
  8.6 1.1 reduce-window.6
  9.7 0.2 slice_reduce_fusion
  10.0 0.1 fusion.34
  10.0 0.7 compare_select_fusion
  10.7 1.4 fusion.27
  12.1 4.4 %scatter_custom_fusion = bf16[768,768]{1,0:T(8,128)(2,1)} fusion(s32[512]{0:T(512)S(1)} %compare_select_fusion, bf16[512,768]{1,0:T(8,128)(2,1)} %param.14, f32[512]{0:T(512)S(1)} %add_rsqrt_fusion.1, bf16[]{:T(256)} %constant.197.clone.1), kind=kCustom, calls=%fused_computation.56 | custom fusion | flops 1179648 | bytes 1968130 | tf_op jit(solution)/shard_map/scatter | solution.py:57
  16.5 7.3 %all-to-all-start = ((bf16[8,96,768]{2,1,0:T(8,128)(2,1)}), bf16[8,96,768]{2,1,0:T(8,128)(2,1)S(1)}, u32[]{:S(2)}, u32[]{:S(2)}) async-start(bf16[8,96,768]{2,1,0:T(8,128)(2,1)} %bitcast.3), calls=%async_computation | async-start | bytes 2359296 | tf_op jit(solution)/shard_map/all_to_all | solution.py:65
  23.8 0.4 fusion.25
  24.2 1.5 fusion.26
  25.8 4.7 %collective-permute-start.1 = (bf16[1024,768]{1,0:T(8,128)(2,1)}, bf16[1024,768]{1,0:T(8,128)(2,1)}, u32[]{:S(2)}, u32[]{:S(2)}) collective-permute-start(bf16[1024,768]{1,0:T(8,128)(2,1)} %fusion.26), channel_id=1, source_target_pairs={{0,14},{2,0},{4,2},{6,4},{8,6},{10,8},{12,10},{14,12},{1,15},{3,1}... | collective-permute-start | bytes 4718600 | tf_op jit(solution)/shard_map/ppermute | solution.py:18
  30.4 23.3 %all-to-all-done = bf16[8,96,768]{2,1,0:T(8,128)(2,1)S(1)} async-done(((bf16[8,96,768]{2,1,0:T(8,128)(2,1)}), bf16[8,96,768]{2,1,0:T(8,128)(2,1)S(1)}, u32[]{:S(2)}, u32[]{:S(2)}) %all-to-all-start) | async-done | bytes 1179680 | tf_op jit(solution)/shard_map/all_to_all | solution.py:65
  53.8 1.1 copy-done.1
  54.9 22.2 %collective-permute-done.1 = bf16[1024,768]{1,0:T(8,128)(2,1)} collective-permute-done((bf16[1024,768]{1,0:T(8,128)(2,1)}, bf16[1024,768]{1,0:T(8,128)(2,1)}, u32[]{:S(2)}, u32[]{:S(2)}) %collective-permute-start.1) | collective-permute-done | bytes 1572896 | tf_op jit(solution)/shard_map/ppermute | solution.py:18
  77.1 9.4 %collective-permute-start.3 = (bf16[1024,768]{1,0:T(8,128)(2,1)}, bf16[1024,768]{1,0:T(8,128)(2,1)}, u32[]{:S(2)}, u32[]{:S(2)}) collective-permute-start(bf16[1024,768]{1,0:T(8,128)(2,1)} %collective-permute-done.1), channel_id=1, source_target_pairs={{0,14},{2,0},{4,2},{6,4},{8,6},{10,8},{12,10},{14,12},{1,15},{3,1}... | collective-permute-start | bytes 4718600 | tf_op jit(solution)/shard_map/ppermute | solution.py:18
  86.6 3.8 %scatter_custom_fusion.1 = bf16[768]{0:T(1024)(128)(2,1)S(1)} fusion(s32[512]{0:T(512)S(1)} %compare_select_fusion, bf16[512]{0:T(512)(128)(2,1)S(1)} %broadcast.118, bf16[]{:T(256)} %constant.197.clone.1), kind=kCustom, calls=%fused_computation.79 | custom fusion | bytes 1538 | tf_op jit(solution)/shard_map/scatter | solution.py:62
  90.4 0.7 all_to_all.20
  91.0 4.9 %all-to-all-start.1 = ((bf16[8,1,96]{2,1,0:T(2,128)(2,1)}), bf16[8,1,96]{2,1,0:T(2,128)(2,1)S(1)}, u32[]{:S(2)}, u32[]{:S(2)}) async-start(bf16[8,1,96]{2,1,0:T(2,128)(2,1)} %all_to_all.20), calls=%async_computation.1 | async-start | bytes 8192 | tf_op jit(solution)/shard_map/all_to_all | solution.py:72
  96.0 0.6 dynamic-slice
  97.1 26.5 %all-to-all-done.1 = bf16[8,1,96]{2,1,0:T(2,128)(2,1)S(1)} async-done(((bf16[8,1,96]{2,1,0:T(2,128)(2,1)}), bf16[8,1,96]{2,1,0:T(2,128)(2,1)S(1)}, u32[]{:S(2)}, u32[]{:S(2)}) %all-to-all-start.1) | async-done | bytes 1568 | tf_op jit(solution)/shard_map/all_to_all | solution.py:72
  123.6 0.1 reshape.127
  123.7 1.8 all-gather
  125.6 2.3 collective-permute-start.5
  127.9 8.9 %while.75 = (s32[]{:T(128)}, f32[1024]{0:T(1024)S(1)}, f32[3,512]{1,0:T(4,128)S(1)}, bf16[3,512,768]{2,1,0:T(8,128)(2,1)}, bf16[1024,768]{1,0:T(8,128)(2,1)}, /*index=5*/f32[3,512]{1,0:T(4,128)S(1)}, s32[]{:T(128)}, s32[]{:T(128)}) while((s32[]{:T(128)}, f32[1024]{0:T(1024)S(1)}, f32[3,512]{1,0:T(4,128)S(1)}, ...), condition=%wide.region_10.11_spmd.clone, body=%wide.region_7.10_spmd.clone.sunk | while | flops 807928320 | bytes 2388083 | solution.py:41
  127.9 2.9 %fusion.57 = (f32[512]{0:T(512)S(1)}, f32[1024]{0:T(1024)S(1)}) fusion(f32[512]{0:T(512)S(1)} %bitcast.100, bf16[1024,768]{1,0:T(8,128)(2,1)} %get-tuple-element.802, bf16[3,512,768]{2,1,0:T(8,128)(2,1)} %get-tuple-element.801, s32[]{:T(128)S(6)} %copy.14), kind=kOutput, calls=%fused_computation.5.clone.1 | convolution fusion | flops 807926272 | bytes 2367492 | tf_op jit(solution)/shard_map/while/body/eval_jaxpr/vd,rd->vr/dot_general | solution.py:37
  130.9 2.9 %fusion.57 = (f32[512]{0:T(512)S(1)}, f32[1024]{0:T(1024)S(1)}) fusion(f32[512]{0:T(512)S(1)} %bitcast.100, bf16[1024,768]{1,0:T(8,128)(2,1)} %get-tuple-element.802, bf16[3,512,768]{2,1,0:T(8,128)(2,1)} %get-tuple-element.801, s32[]{:T(128)S(6)} %copy.14), kind=kOutput, calls=%fused_computation.5.clone.1 | convolution fusion | flops 807926272 | bytes 2367492 | tf_op jit(solution)/shard_map/while/body/eval_jaxpr/vd,rd->vr/dot_general | solution.py:37
  133.9 2.9 %fusion.57 = (f32[512]{0:T(512)S(1)}, f32[1024]{0:T(1024)S(1)}) fusion(f32[512]{0:T(512)S(1)} %bitcast.100, bf16[1024,768]{1,0:T(8,128)(2,1)} %get-tuple-element.802, bf16[3,512,768]{2,1,0:T(8,128)(2,1)} %get-tuple-element.801, s32[]{:T(128)S(6)} %copy.14), kind=kOutput, calls=%fused_computation.5.clone.1 | convolution fusion | flops 807926272 | bytes 2367492 | tf_op jit(solution)/shard_map/while/body/eval_jaxpr/vd,rd->vr/dot_general | solution.py:37
  136.9 1.1 collective-permute-start
  137.9 8.9 %while.76 = (s32[]{:T(128)}, f32[1024]{0:T(1024)S(1)}, f32[3,512]{1,0:T(4,128)S(1)}, bf16[3,512,768]{2,1,0:T(8,128)(2,1)}, bf16[1024,768]{1,0:T(8,128)(2,1)}, /*index=5*/f32[3,512]{1,0:T(4,128)S(1)}, s32[]{:T(128)}, s32[]{:T(128)}) while((s32[]{:T(128)}, f32[1024]{0:T(1024)S(1)}, f32[3,512]{1,0:T(4,128)S(1)}, ...), condition=%wide.region_14.15_spmd.clone, body=%wide.region_11.14_spmd.clone.sunk | while | flops 807928320 | bytes 2388083 | solution.py:41
  137.9 2.9 %fusion.59 = (f32[512]{0:T(512)S(1)}, f32[1024]{0:T(1024)S(1)}) fusion(f32[512]{0:T(512)S(1)} %bitcast.101, bf16[1024,768]{1,0:T(8,128)(2,1)} %get-tuple-element.826, bf16[3,512,768]{2,1,0:T(8,128)(2,1)} %get-tuple-element.825, s32[]{:T(128)S(6)} %copy.23), kind=kOutput, calls=%fused_computation.14.clone.1 | convolution fusion | flops 807926272 | bytes 2367492 | tf_op jit(solution)/shard_map/while/body/eval_jaxpr/vd,rd->vr/dot_general | solution.py:37
  140.9 2.9 %fusion.59 = (f32[512]{0:T(512)S(1)}, f32[1024]{0:T(1024)S(1)}) fusion(f32[512]{0:T(512)S(1)} %bitcast.101, bf16[1024,768]{1,0:T(8,128)(2,1)} %get-tuple-element.826, bf16[3,512,768]{2,1,0:T(8,128)(2,1)} %get-tuple-element.825, s32[]{:T(128)S(6)} %copy.23), kind=kOutput, calls=%fused_computation.14.clone.1 | convolution fusion | flops 807926272 | bytes 2367492 | tf_op jit(solution)/shard_map/while/body/eval_jaxpr/vd,rd->vr/dot_general | solution.py:37
  143.9 2.9 %fusion.59 = (f32[512]{0:T(512)S(1)}, f32[1024]{0:T(1024)S(1)}) fusion(f32[512]{0:T(512)S(1)} %bitcast.101, bf16[1024,768]{1,0:T(8,128)(2,1)} %get-tuple-element.826, bf16[3,512,768]{2,1,0:T(8,128)(2,1)} %get-tuple-element.825, s32[]{:T(128)S(6)} %copy.23), kind=kOutput, calls=%fused_computation.14.clone.1 | convolution fusion | flops 807926272 | bytes 2367492 | tf_op jit(solution)/shard_map/while/body/eval_jaxpr/vd,rd->vr/dot_general | solution.py:37
  146.8 15.6 %collective-permute-done = f32[1024]{0:T(1024)S(1)} collective-permute-done((f32[1024]{0:T(1024)S(1)}, f32[1024]{0:T(1024)S(1)}, u32[]{:S(2)}, u32[]{:S(2)}) %collective-permute-start) | collective-permute-done | bytes 4128 | tf_op jit(solution)/shard_map/ppermute | solution.py:18
  162.5 5.0 %collective-permute-start.2 = (f32[1024]{0:T(1024)S(1)}, f32[1024]{0:T(1024)S(1)}, u32[]{:S(2)}, u32[]{:S(2)}) collective-permute-start(f32[1024]{0:T(1024)S(1)} %add.149), channel_id=1, source_target_pairs={{0,14},{2,0},{4,2},{6,4},{8,6},{10,8},{12,10},{14,12},{1,15},{3,1}... | collective-permute-start | bytes 12296 | tf_op jit(solution)/shard_map/ppermute | solution.py:18
  167.5 8.9 %while.77 = (s32[]{:T(128)}, f32[1024]{0:T(1024)S(1)}, f32[3,512]{1,0:T(4,128)S(1)}, bf16[3,512,768]{2,1,0:T(8,128)(2,1)}, bf16[1024,768]{1,0:T(8,128)(2,1)}, /*index=5*/f32[3,512]{1,0:T(4,128)S(1)}, s32[]{:T(128)}, s32[]{:T(128)}) while((s32[]{:T(128)}, f32[1024]{0:T(1024)S(1)}, f32[3,512]{1,0:T(4,128)S(1)}, ...), condition=%wide.region_18.19_spmd.clone, body=%wide.region_15.18_spmd.clone.sunk | while | flops 807928320 | bytes 2388083 | solution.py:41
  167.5 2.9 %fusion.61 = (f32[512]{0:T(512)S(1)}, f32[1024]{0:T(1024)S(1)}) fusion(f32[512]{0:T(512)S(1)} %bitcast.102, bf16[1024,768]{1,0:T(8,128)(2,1)} %get-tuple-element.850, bf16[3,512,768]{2,1,0:T(8,128)(2,1)} %get-tuple-element.849, s32[]{:T(128)S(6)} %copy.32), kind=kOutput, calls=%fused_computation.23.clone.1 | convolution fusion | flops 807926272 | bytes 2367492 | tf_op jit(solution)/shard_map/while/body/eval_jaxpr/vd,rd->vr/dot_general | solution.py:37
  170.4 2.9 %fusion.61 = (f32[512]{0:T(512)S(1)}, f32[1024]{0:T(1024)S(1)}) fusion(f32[512]{0:T(512)S(1)} %bitcast.102, bf16[1024,768]{1,0:T(8,128)(2,1)} %get-tuple-element.850, bf16[3,512,768]{2,1,0:T(8,128)(2,1)} %get-tuple-element.849, s32[]{:T(128)S(6)} %copy.32), kind=kOutput, calls=%fused_computation.23.clone.1 | convolution fusion | flops 807926272 | bytes 2367492 | tf_op jit(solution)/shard_map/while/body/eval_jaxpr/vd,rd->vr/dot_general | solution.py:37
  173.4 2.9 %fusion.61 = (f32[512]{0:T(512)S(1)}, f32[1024]{0:T(1024)S(1)}) fusion(f32[512]{0:T(512)S(1)} %bitcast.102, bf16[1024,768]{1,0:T(8,128)(2,1)} %get-tuple-element.850, bf16[3,512,768]{2,1,0:T(8,128)(2,1)} %get-tuple-element.849, s32[]{:T(128)S(6)} %copy.32), kind=kOutput, calls=%fused_computation.23.clone.1 | convolution fusion | flops 807926272 | bytes 2367492 | tf_op jit(solution)/shard_map/while/body/eval_jaxpr/vd,rd->vr/dot_general | solution.py:37
  176.4 0.1 collective-permute-start.4
  176.5 0.4 collective-permute-start.7
  176.8 8.9 %while.78 = (s32[]{:T(128)}, f32[1024]{0:T(1024)S(1)}, f32[3,512]{1,0:T(4,128)S(1)}, bf16[3,512,768]{2,1,0:T(8,128)(2,1)}, bf16[1024,768]{1,0:T(8,128)(2,1)}, /*index=5*/f32[3,512]{1,0:T(4,128)S(1)}, s32[]{:T(128)}, s32[]{:T(128)}) while((s32[]{:T(128)}, f32[1024]{0:T(1024)S(1)}, f32[3,512]{1,0:T(4,128)S(1)}, ...), condition=%wide.region_22.23_spmd.clone, body=%wide.region_19.22_spmd.clone.sunk | while | flops 807928320 | bytes 2388083 | solution.py:41
  176.9 2.9 %fusion.63 = (f32[512]{0:T(512)S(1)}, f32[1024]{0:T(1024)S(1)}) fusion(f32[512]{0:T(512)S(1)} %bitcast.103, bf16[1024,768]{1,0:T(8,128)(2,1)} %get-tuple-element.874, bf16[3,512,768]{2,1,0:T(8,128)(2,1)} %get-tuple-element.873, s32[]{:T(128)S(6)} %copy.41), kind=kOutput, calls=%fused_computation.32.clone.1 | convolution fusion | flops 807926272 | bytes 2367492 | tf_op jit(solution)/shard_map/while/body/eval_jaxpr/vd,rd->vr/dot_general | solution.py:37
  179.8 2.9 %fusion.63 = (f32[512]{0:T(512)S(1)}, f32[1024]{0:T(1024)S(1)}) fusion(f32[512]{0:T(512)S(1)} %bitcast.103, bf16[1024,768]{1,0:T(8,128)(2,1)} %get-tuple-element.874, bf16[3,512,768]{2,1,0:T(8,128)(2,1)} %get-tuple-element.873, s32[]{:T(128)S(6)} %copy.41), kind=kOutput, calls=%fused_computation.32.clone.1 | convolution fusion | flops 807926272 | bytes 2367492 | tf_op jit(solution)/shard_map/while/body/eval_jaxpr/vd,rd->vr/dot_general | solution.py:37
  182.7 0.1 dynamic_update_slice.44
  182.8 2.9 %fusion.63 = (f32[512]{0:T(512)S(1)}, f32[1024]{0:T(1024)S(1)}) fusion(f32[512]{0:T(512)S(1)} %bitcast.103, bf16[1024,768]{1,0:T(8,128)(2,1)} %get-tuple-element.874, bf16[3,512,768]{2,1,0:T(8,128)(2,1)} %get-tuple-element.873, s32[]{:T(128)S(6)} %copy.41), kind=kOutput, calls=%fused_computation.32.clone.1 | convolution fusion | flops 807926272 | bytes 2367492 | tf_op jit(solution)/shard_map/while/body/eval_jaxpr/vd,rd->vr/dot_general | solution.py:37
  185.8 0.3 collective-permute-start.6
  186.1 26.3 %collective-permute-done.7 = bf16[1024,768]{1,0:T(8,128)(2,1)S(1)} collective-permute-done((bf16[1024,768]{1,0:T(8,128)(2,1)}, bf16[1024,768]{1,0:T(8,128)(2,1)S(1)}, u32[]{:S(2)}, u32[]{:S(2)}) %collective-permute-start.7) | collective-permute-done | bytes 1572896 | tf_op jit(solution)/shard_map/ppermute | solution.py:18
  212.4 7.4 %while.79 = (s32[]{:T(128)}, f32[1024]{0:T(1024)S(1)}, f32[3,512]{1,0:T(4,128)S(1)}, bf16[3,512,768]{2,1,0:T(8,128)(2,1)}, bf16[1024,768]{1,0:T(8,128)(2,1)S(1)}...) while((s32[]{:T(128)}, f32[1024]{0:T(1024)S(1)}, f32[3,512]{1,0:T(4,128)S(1)}, ...), condition=%wide.region_26.27_spmd.clone, body=%wide.region_23.26_spmd.clone.sunk | while | flops 807928320 | bytes 2388083 | solution.py:41
  212.4 2.4 fusion.65
  214.9 2.4 fusion.65
  217.3 2.4 fusion.65
  219.8 0.1 collective-permute-start.8
  219.9 2.5 %all-reduce = f32[1536]{0:T(1024)S(1)} all-reduce(f32[1536]{0:T(1024)S(1)} %add.157), channel_id=2, replica_groups=mesh['groups'=2,'blk'=8,'rep'=2] {'rep'}, use_global_device_ids=true, to_apply=%region_27.28.clone | all-reduce | flops 1536 | bytes 12288
  222.4 0.1 dynamic-slice.1
  222.5 0.7 all_to_all.18
  223.1 6.0 %all-to-all-start.2 = ((f32[8,1,96]{2,1,0:T(1,128)}), f32[8,1,96]{2,1,0:T(1,128)S(1)}, u32[]{:S(2)}, u32[]{:S(2)}) async-start(f32[8,1,96]{2,1,0:T(1,128)} %all_to_all.18), calls=%async_computation.2 | async-start | bytes 8192 | tf_op jit(solution)/shard_map/all_to_all | solution.py:95
  229.1 0.6 log1p.6
  229.7 5.9 %all-to-all-done.2 = f32[8,1,96]{2,1,0:T(1,128)S(1)} async-done(((f32[8,1,96]{2,1,0:T(1,128)}), f32[8,1,96]{2,1,0:T(1,128)S(1)}, u32[]{:S(2)}, u32[]{:S(2)}) %all-to-all-start.2) | async-done | bytes 3104 | tf_op jit(solution)/shard_map/all_to_all | solution.py:95
  235.6 0.5 broadcast.194
  236.1 0.7 reduce.8
  236.8 0.1 reshape.97
  236.9 2.3 gather_fusion
  239.1 0.6 log1p.7
  (84 shorter events, 1.2 us)
Async XLA Ops:
  12.1 11.7 %copy-start = (bf16[1024,768]{1,0:T(8,128)(2,1)S(1)}, bf16[1024,768]{1,0:T(8,128)(2,1)}, u32[]{:S(2)}) copy-start(bf16[1024,768]{1,0:T(8,128)(2,1)} %param.13) | copy-start | bytes 4718596
  16.5 37.3 %all-to-all-start = ((bf16[8,96,768]{2,1,0:T(8,128)(2,1)}), bf16[8,96,768]{2,1,0:T(8,128)(2,1)S(1)}, u32[]{:S(2)}, u32[]{:S(2)}) async-start(bf16[8,96,768]{2,1,0:T(8,128)(2,1)} %bitcast.3), calls=%async_computation | async-start | bytes 2359296 | tf_op jit(solution)/shard_map/all_to_all | solution.py:65
  23.8 104.1 %all-gather.3.cloned.1.call-start = ((), (), s32[]{:S(2)}) async-start(), calls=%async_computation.3 | async-start | bytes 3538944 | tf_op jit(solution)/shard_map/all_gather | solution.py:77
  24.2 71.8 %copy-start.2 = (u32[32]{0:T(128)S(1)}, u32[32]{0:T(128)}, u32[]{:S(2)}) copy-start(u32[32]{0:T(128)} %constant.208) | copy-start | bytes 388
  25.8 51.4 %collective-permute-start.1 = (bf16[1024,768]{1,0:T(8,128)(2,1)}, bf16[1024,768]{1,0:T(8,128)(2,1)}, u32[]{:S(2)}, u32[]{:S(2)}) collective-permute-start(bf16[1024,768]{1,0:T(8,128)(2,1)} %fusion.26), channel_id=1, source_target_pairs={{0,14},{2,0},{4,2},{6,4},{8,6},{10,8},{12,10},{14,12},{1,15},{3,1}... | collective-permute-start | bytes 4718600 | tf_op jit(solution)/shard_map/ppermute | solution.py:18
  53.8 1.1 copy-start.1
  77.1 48.4 %collective-permute-start.3 = (bf16[1024,768]{1,0:T(8,128)(2,1)}, bf16[1024,768]{1,0:T(8,128)(2,1)}, u32[]{:S(2)}, u32[]{:S(2)}) collective-permute-start(bf16[1024,768]{1,0:T(8,128)(2,1)} %collective-permute-done.1), channel_id=1, source_target_pairs={{0,14},{2,0},{4,2},{6,4},{8,6},{10,8},{12,10},{14,12},{1,15},{3,1}... | collective-permute-start | bytes 4718600 | tf_op jit(solution)/shard_map/ppermute | solution.py:18
  91.0 32.6 %all-to-all-start.1 = ((bf16[8,1,96]{2,1,0:T(2,128)(2,1)}), bf16[8,1,96]{2,1,0:T(2,128)(2,1)S(1)}, u32[]{:S(2)}, u32[]{:S(2)}) async-start(bf16[8,1,96]{2,1,0:T(2,128)(2,1)} %all_to_all.20), calls=%async_computation.1 | async-start | bytes 8192 | tf_op jit(solution)/shard_map/all_to_all | solution.py:72
  125.6 50.9 %collective-permute-start.5 = (bf16[1024,768]{1,0:T(8,128)(2,1)}, bf16[1024,768]{1,0:T(8,128)(2,1)}, u32[]{:S(2)}, u32[]{:S(2)}) collective-permute-start(bf16[1024,768]{1,0:T(8,128)(2,1)} %collective-permute-done.3), channel_id=1, source_target_pairs={{0,14},{2,0},{4,2},{6,4},{8,6},{10,8},{12,10},{14,12},{1,15},{3,1}... | collective-permute-start | bytes 4718600 | tf_op jit(solution)/shard_map/ppermute | solution.py:18
  136.9 25.6 %collective-permute-start = (f32[1024]{0:T(1024)S(1)}, f32[1024]{0:T(1024)S(1)}, u32[]{:S(2)}, u32[]{:S(2)}) collective-permute-start(f32[1024]{0:T(1024)S(1)} %get-tuple-element.392), channel_id=1, source_target_pairs={{0,14},{2,0},{4,2},{6,4},{8,6},{10,8},{12,10},{14,12},{1,15},{3,1}... | collective-permute-start | bytes 12296 | tf_op jit(solution)/shard_map/ppermute | solution.py:18
  162.5 13.9 %collective-permute-start.2 = (f32[1024]{0:T(1024)S(1)}, f32[1024]{0:T(1024)S(1)}, u32[]{:S(2)}, u32[]{:S(2)}) collective-permute-start(f32[1024]{0:T(1024)S(1)} %add.149), channel_id=1, source_target_pairs={{0,14},{2,0},{4,2},{6,4},{8,6},{10,8},{12,10},{14,12},{1,15},{3,1}... | collective-permute-start | bytes 12296 | tf_op jit(solution)/shard_map/ppermute | solution.py:18
  176.4 9.4 %collective-permute-start.4 = (f32[1024]{0:T(1024)S(1)}, f32[1024]{0:T(1024)S(1)}, u32[]{:S(2)}, u32[]{:S(2)}) collective-permute-start(f32[1024]{0:T(1024)S(1)} %add.150), channel_id=1, source_target_pairs={{0,14},{2,0},{4,2},{6,4},{8,6},{10,8},{12,10},{14,12},{1,15},{3,1}... | collective-permute-start | bytes 12296 | tf_op jit(solution)/shard_map/ppermute | solution.py:18
  176.5 35.9 %collective-permute-start.7 = (bf16[1024,768]{1,0:T(8,128)(2,1)}, bf16[1024,768]{1,0:T(8,128)(2,1)S(1)}, u32[]{:S(2)}, u32[]{:S(2)}) collective-permute-start(bf16[1024,768]{1,0:T(8,128)(2,1)} %collective-permute-done.5), channel_id=1, source_target_pairs={{0,14},{2,0},{4,2},{6,4},{8,6},{10,8},{12,10},{14,12},{1,15},{3,1}... | collective-permute-start | bytes 4718600 | tf_op jit(solution)/shard_map/ppermute | solution.py:18
  185.8 34.0 %collective-permute-start.6 = (f32[1024]{0:T(1024)S(1)}, f32[1024]{0:T(1024)S(1)}, u32[]{:S(2)}, u32[]{:S(2)}) collective-permute-start(f32[1024]{0:T(1024)S(1)} %add.151), channel_id=1, source_target_pairs={{0,14},{2,0},{4,2},{6,4},{8,6},{10,8},{12,10},{14,12},{1,15},{3,1}... | collective-permute-start | bytes 12296 | tf_op jit(solution)/shard_map/ppermute | solution.py:18
  219.8 9.3 %collective-permute-start.8 = (f32[1024]{0:T(1024)S(1)}, f32[1024]{0:T(1024)S(1)}, u32[]{:S(2)}, u32[]{:S(2)}) collective-permute-start(f32[1024]{0:T(1024)S(1)} %add.152), channel_id=1, source_target_pairs={{0,8},{2,10},{4,12},{6,14},{8,0},{10,2},{12,4},{14,6},{1,9},{3,11}... | collective-permute-start | bytes 12296 | tf_op jit(solution)/shard_map/ppermute | solution.py:18
  223.1 12.4 %all-to-all-start.2 = ((f32[8,1,96]{2,1,0:T(1,128)}), f32[8,1,96]{2,1,0:T(1,128)S(1)}, u32[]{:S(2)}, u32[]{:S(2)}) async-start(f32[8,1,96]{2,1,0:T(1,128)} %all_to_all.18), calls=%async_computation.2 | async-start | bytes 8192 | tf_op jit(solution)/shard_map/all_to_all | solution.py:95
Sparse Core Ops, SparseCore 0:
  55.0 41.4 all-gather.2
where the time goes:
time: 248 us; the launch traced here: 247 us
  waiting for transfers between devices  120 us (48%)
  matrix products  41.6 us (17%)
  starting transfers between devices  41.5 us (17%)
  between operations  14.8 us (6%)
  local copies, waits for them, and re-layouts  12.1 us (5%)
  other arithmetic  11.8 us (5%)
  blocking collectives  4.32 us (2%)
    ppermute x9, waiting for transfers between devices, shifted(): return lax.ppermute(value, axis, pairs)  64.2 us
    dot_general x15, matrix products, tile_sums(): jnp.einsum('vd,rd->vr', visit_tile, residents, preferred_element_type=jnp...  41.6 us
    all_to_all x1, waiting for transfers between devices, on_device(): lax.all_to_all(filled.reshape(cycle_size, slot_count), 'blk', split_axis=...  26.5 us
    all_to_all x1, waiting for transfers between devices, on_device(): lax.all_to_all(outgoing.reshape(cycle_size, slot_count, columns), 'blk',...  23.3 us
    ppermute x9, starting transfers between devices, shifted(): return lax.ppermute(value, axis, pairs)  23.3 us
    all_to_all x1, starting transfers between devices, on_device(): lax.all_to_all(outgoing.reshape(cycle_size, slot_count, columns), 'blk',...  7.31 us
    all_to_all x1, starting transfers between devices, on_device(): lax.all_to_all(own_sums.reshape(cycle_size, slot_count), 'blk', split_axi...  5.96 us
    all_to_all x1, waiting for transfers between devices, on_device(): lax.all_to_all(own_sums.reshape(cycle_size, slot_count), 'blk', split_axi...  5.87 us
  transfers between devices with their start and end apart: 13, of which 6 were waited for; matrix products, arithmetic and copies ran while one was open for 20% of the time, Pallas kernels for 0%

commit v1 on v0

--- a/solution.py
+++ b/solution.py
@@ -1,6 +1,11 @@
+import functools
+import math
+
 import jax
 import jax.numpy as jnp
 from jax import lax
+from jax.experimental import pallas as pl
+from jax.experimental.pallas import tpu as pltpu
 from jax.sharding import PartitionSpec as P
 
 INGEST_DEV = 512
@@ -99,6 +104,296 @@
     return (jnp.log1p(resident_total), jnp.log1p(density))
 
 
+PAIR = 2
+LANES = 128
+SUBLANES = 8
+INGEST_CHUNK = 256
+RESIDENT_CHUNK = 256
+TILE = 512
+MESH = pl.DeviceIdType.MESH
+
+
+def dense_kernel(
+    cycle, ids_ref, ingest_ref, resident_ref, resident_out, ingest_out,
+    rows, bank, ids, by_resident, by_ingest, resident_sums, ingest_sums, resident_terms, ingest_terms,
+    up_send, down_send, rows_recv, ids_send, ids_recv, peer_send, peer_recv, core_send, core_recv,
+    relay_send, relay_recv, part_send, part_recv, term_send, term_recv,
+):
+    line_size = cycle // PAIR
+    me = lax.axis_index("blk")
+    core = lax.axis_index("rep")
+    line, side = me // PAIR, me % PAIR
+    chunks = ingest_ref.shape[0] // INGEST_CHUNK
+    held = resident_ref.shape[0]
+    pieces = held // RESIDENT_CHUNK
+    tiles = held // TILE
+    steps = (line_size - 1) * chunks
+
+    def device(at_line, at_side, at_core):
+        return {"blk": at_line * PAIR + at_side, "rep": at_core}
+
+    sibling = device(line, side, 1 - core)
+    peer = device(line, 1 - side, core)
+    across = device(line, 1 - side, 1 - core)
+
+    def remote(source, target, send, recv, where):
+        return pltpu.make_async_remote_copy(
+            src_ref=source, dst_ref=target, send_sem=send, recv_sem=recv, device_id=where, device_id_type=MESH
+        )
+
+    def up_copy(c):
+        return remote(rows.at[c], rows.at[c], up_send.at[c], rows_recv.at[c], device(line + 1, side, core))
+
+    def down_copy(c):
+        return remote(rows.at[c], rows.at[c], down_send.at[c], rows_recv.at[c], device(line - 1, side, core))
+
+    def peer_copy(m):
+        return remote(
+            bank.at[pl.ds(m * RESIDENT_CHUNK, RESIDENT_CHUNK)],
+            bank.at[pl.ds(2 * held + m * RESIDENT_CHUNK, RESIDENT_CHUNK)],
+            peer_send.at[m], peer_recv.at[m], peer,
+        )
+
+    def relay_copy(m):
+        return remote(
+            bank.at[pl.ds(2 * held + m * RESIDENT_CHUNK, RESIDENT_CHUNK)],
+            bank.at[pl.ds(3 * held + m * RESIDENT_CHUNK, RESIDENT_CHUNK)],
+            relay_send.at[m], relay_recv.at[m], sibling,
+        )
+
+    core_copy = remote(bank.at[pl.ds(0, held)], bank.at[pl.ds(held, held)], core_send, core_recv, sibling)
+
+    def ids_copy(other):
+        mine = ids.at[pl.ds(line * chunks, chunks)]
+        return remote(mine, mine, ids_send.at[other], ids_recv.at[line], device(other, side, core))
+
+    def ids_arrival(other):
+        theirs = ids.at[pl.ds(other * chunks, chunks)]
+        return remote(theirs, theirs, ids_send.at[other], ids_recv.at[other], device(other, side, core))
+
+    def term_copy(other):
+        return remote(
+            ingest_sums.at[pl.ds(other * chunks, chunks)], ingest_terms.at[pl.ds(line * chunks, chunks)],
+            term_send.at[other], term_recv.at[line], device(other, side, core),
+        )
+
+    def term_arrival(other):
+        return remote(
+            ingest_sums.at[pl.ds(other * chunks, chunks)], ingest_terms.at[pl.ds(other * chunks, chunks)],
+            term_send.at[other], term_recv.at[other], device(other, side, core),
+        )
+
+    def part_copy(slot):
+        return remote(
+            resident_sums.at[slot], resident_terms.at[slot], part_send.at[slot], part_recv.at[slot],
+            (None, sibling, peer, across)[slot],
+        )
+
+    barrier = pltpu.get_barrier_semaphore()
+    for where in (sibling, peer, across):
+        pl.semaphore_signal(barrier, inc=1, device_id=where, device_id_type=MESH)
+    for hop in range(1, line_size):
+        pl.semaphore_signal(
+            barrier, inc=1, device_id=device((line + hop) % line_size, side, core), device_id_type=MESH
+        )
+
+    def unit(block):
+        values = block.astype(jnp.float32)
+        squares = jnp.sum(values * values, axis=-1, keepdims=True) + epsilon
+        return (values * lax.rsqrt(squares)).astype(jnp.bfloat16)
+
+    for j in range(chunks):
+        rows[line * chunks + j] = unit(ingest_ref[j * INGEST_CHUNK:(j + 1) * INGEST_CHUNK, :])
+        ids[line * chunks + j] = ids_ref[j]
+    pl.semaphore_wait(barrier, line_size + 2)
+    for j in range(chunks):
+        @pl.when(line + 1 < line_size)
+        def _():
+            up_copy(line * chunks + j).start()
+
+        @pl.when(line > 0)
+        def _():
+            down_copy(line * chunks + j).start()
+    for hop in range(1, line_size):
+        ids_copy((line + hop) % line_size).start()
+
+    @pl.loop(0, pieces)
+    def _(m):
+        part = pl.ds(m * RESIDENT_CHUNK, RESIDENT_CHUNK)
+        bank[part, :] = unit(resident_ref[part, :])
+
+    for m in range(pieces):
+        peer_copy(m).start()
+    core_copy.start()
+    by_resident[...] = jnp.zeros_like(by_resident)
+    by_ingest[...] = jnp.zeros_like(by_ingest)
+    for hop in range(1, line_size):
+        ids_arrival((line + hop) % line_size).wait_recv()
+
+    scale = math.log2(math.e) / temper
+    span = CL_OWN * cycle
+
+    def work(c, first, last):
+        @pl.loop(first, last)
+        def _(tile):
+            part = pl.ds(tile * TILE, TILE)
+            position = line * PAIR + jnp.where(tile < 2 * tiles, side, 1 - side)
+            gap = (position + 1) * CL_OWN - 1 - ids[c]
+            gap = jnp.where(gap < 0, gap + span, gap)
+            bias = jnp.where(gap < CL_OWN * (CYCLE_STEPS + 1), -scale, -1e30)
+            scores = lax.dot_general(
+                bank[part, :], rows[c], (((1,), (1,)), ((), ())), preferred_element_type=jnp.float32
+            )
+            kernel = jnp.exp2(scores * scale + bias)
+            by_ingest[c] += jnp.sum(kernel.reshape(TILE // SUBLANES, SUBLANES, INGEST_CHUNK), axis=0)
+            folded = kernel[:, :LANES]
+            for n in range(1, INGEST_CHUNK // LANES):
+                folded = folded + kernel[:, n * LANES:(n + 1) * LANES]
+            by_resident[part, :] += folded
+
+    @pl.loop(0, 2)
+    def _(half):
+        @pl.when(half == 1)
+        def _():
+            core_copy.wait_recv()
+
+        @pl.loop(0, chunks)
+        def _(j):
+            work(line * chunks + j, half * tiles, (half + 1) * tiles)
+
+    @pl.loop(0, steps)
+    def _(step):
+        hop, j = step // chunks + 1, step % chunks
+
+        @pl.when(line - hop >= 0)
+        def _():
+            c = (line - hop) * chunks + j
+            up_copy(c).wait_recv()
+
+            @pl.when(line + 1 < line_size)
+            def _():
+                up_copy(c).start()
+
+        @pl.when(line + hop < line_size)
+        def _():
+            c = (line + hop) * chunks + j
+            down_copy(c).wait_recv()
+
+            @pl.when(line > 0)
+            def _():
+                down_copy(c).start()
+
+        @pl.when(step < pieces)
+        def _():
+            peer_copy(step).wait_recv()
+            relay_copy(step).start()
+
+        @pl.loop(0, 2)
+        def _(way):
+            other = line + (2 * way - 1) * hop
+
+            @pl.when((other >= 0) & (other < line_size))
+            def _():
+                work(other * chunks + j, 0, jnp.where(step < pieces, 2 * tiles, 4 * tiles))
+
+        @pl.when(step == pieces - 1)
+        def _():
+            for m in range(pieces):
+                relay_copy(m).wait_recv()
+
+            @pl.loop(0, line_size * chunks)
+            def _(c):
+                away = jnp.abs(c // chunks - line)
+                arrived = (away - 1) * chunks + c % chunks
+
+                @pl.when((away == 0) | (arrived < pieces))
+                def _():
+                    work(c, 2 * tiles, 4 * tiles)
+
+    ingest_sums[...] = jnp.sum(by_ingest[...], axis=1, keepdims=True)
+
+    def gather_slot(slot):
+        block = by_resident[slot * held:(slot + 1) * held, :]
+        resident_sums[slot] = jnp.sum(block.T, axis=0, keepdims=True)
+
+    for slot in (3, 2, 1):
+        gather_slot(slot)
+    for hop in range(1, line_size):
+        term_copy((line + hop) % line_size).start()
+    gather_slot(0)
+    for slot in (3, 2, 1):
+        part_copy(slot).start()
+
+    for c in range(line_size * chunks):
+        @pl.when((c // chunks <= line) & (line + 1 < line_size))
+        def _():
+            up_copy(c).wait_send()
+
+        @pl.when((c // chunks >= line) & (line > 0))
+        def _():
+            down_copy(c).wait_send()
+    for m in range(pieces):
+        peer_copy(m).wait_send()
+        relay_copy(m).wait_send()
+    core_copy.wait_send()
+
+    resident_total = resident_sums[0]
+    for slot in (1, 2, 3):
+        part_copy(slot).wait()
+        resident_total = resident_total + resident_terms[slot]
+    resident_out[...] = resident_total
+    ingest_total = ingest_sums[pl.ds(line * chunks, chunks)]
+    for hop in range(1, line_size):
+        other = (line + hop) % line_size
+        term_arrival(other).wait_recv()
+        ingest_total = ingest_total + ingest_terms[pl.ds(other * chunks, chunks)]
+    ingest_out[...] = ingest_total
+    for hop in range(1, line_size):
+        other = (line + hop) % line_size
+        ids_copy(other).wait_send()
+        term_copy(other).wait_send()
+
+
+def dense_on_device(cycle, resident, ingest, cluster_ids):
+    held, columns = resident.shape
+    count = ingest.shape[0]
+    chunks = count // INGEST_CHUNK
+    blocks = cycle // PAIR * chunks
+    line_size = cycle // PAIR
+    pieces = held // RESIDENT_CHUNK
+    dma = pltpu.SemaphoreType.DMA
+    vmem = pl.BlockSpec(memory_space=pltpu.VMEM)
+    resident_total, ingest_total = pl.pallas_call(
+        functools.partial(dense_kernel, cycle),
+        out_shape=(
+            jax.ShapeDtypeStruct((1, held), jnp.float32),
+            jax.ShapeDtypeStruct((chunks, 1, INGEST_CHUNK), jnp.float32),
+        ),
+        in_specs=[vmem] * 3,
+        out_specs=(vmem, vmem),
+        scratch_shapes=[
+            pltpu.VMEM((blocks, INGEST_CHUNK, columns), jnp.bfloat16),
+            pltpu.VMEM((4 * held, columns), jnp.bfloat16),
+            pltpu.VMEM((blocks, 1, INGEST_CHUNK), jnp.int32),
+            pltpu.VMEM((4 * held, LANES), jnp.float32),
+            pltpu.VMEM((blocks, SUBLANES, INGEST_CHUNK), jnp.float32),
+            pltpu.VMEM((4, 1, held), jnp.float32),
+            pltpu.VMEM((blocks, 1, INGEST_CHUNK), jnp.float32),
+            pltpu.VMEM((4, 1, held), jnp.float32),
+            pltpu.VMEM((blocks, 1, INGEST_CHUNK), jnp.float32),
+            dma((blocks,)), dma((blocks,)), dma((blocks,)),
+            dma((line_size,)), dma((line_size,)),
+            dma((pieces,)), dma((pieces,)),
+            dma, dma,
+            dma((pieces,)), dma((pieces,)),
+            dma((4,)), dma((4,)),
+            dma((line_size,)), dma((line_size,)),
+        ],
+        compiler_params=pltpu.CompilerParams(collective_id=0, has_side_effects=True),
+    )(cluster_ids.reshape(chunks, 1, INGEST_CHUNK), ingest, resident)
+    return (jnp.log1p(resident_total.reshape(held)), jnp.log1p(ingest_total.reshape(count)))
+
+
 def solution(mesh):
     in_specs = (
         P(("groups", "blk", "rep"), None),
@@ -106,6 +401,9 @@
         P(("groups", "blk", "rep")),
     )
     out_specs = (P(("groups", "blk", "rep")), P(("groups", "blk", "rep")))
+    cycle = mesh.shape["blk"]
+    dense = 2 * (CYCLE_STEPS + 1) >= cycle and cycle % PAIR == 0 and mesh.shape["rep"] == 2
+    body = functools.partial(dense_on_device, cycle) if dense else on_device
     return jax.shard_map(
-        on_device, mesh=mesh, in_specs=in_specs, out_specs=out_specs, check_vma=False
-    )
+        body, mesh=mesh, in_specs=in_specs, out_specs=out_specs, check_vma=False
+    )

time: 248 us -> 75.6 us (0.30)
  waiting for transfers between devices: 120 us -> 0 us
  Pallas kernels: 0 us -> 72.3 us
  matrix products: 41.6 us -> 0 us
  starting transfers between devices: 41.5 us -> 0 us
  between operations: 14.8 us -> 0.64 us
  other arithmetic: 11.8 us -> 0 us
  local copies, waits for them, and re-layouts: 12.1 us -> 2.52 us
  blocking collectives: 4.32 us -> 0 us
    pallas_call x0 -> x1, Pallas kernels: none -> 72.3 us  [dense_on_device(): pl.pallas_call(functools.partial(dense_kernel, cycle), out_shape=(jax.Sha...]
    ppermute x9 -> x0, waiting for transfers between devices: 64.2 us -> none  [shifted(): return lax.ppermute(value, axis, pairs)]
    all_to_all x3 -> x0, waiting for transfers between devices: 55.7 us -> none  [the longest x1 26.5 us: on_device(): lax.all_to_all(filled.reshape(cycle_size, slot_count), 'blk', split_axis=...]
    dot_general x15 -> x0, matrix products: 41.6 us -> none  [tile_sums(): jnp.einsum('vd,rd->vr', visit_tile, residents, preferred_element_type=jnp...]
    ppermute x9 -> x0, starting transfers between devices: 23.3 us -> none  [shifted(): return lax.ppermute(value, axis, pairs)]
    all_to_all x3 -> x0, starting transfers between devices: 18.2 us -> none  [the longest x1 7.31 us: on_device(): lax.all_to_all(outgoing.reshape(cycle_size, slot_count, columns), 'blk',...]
    scatter x1 -> x0, other arithmetic: 4.35 us -> none  [on_device(): jnp.zeros((cycle_size * slot_count, columns), jnp.bfloat16).at[targets]]
    scatter x1 -> x0, local copies, waits for them, and re-layouts: 3.77 us -> none  [on_device(): filled = jnp.zeros((cycle_size * slot_count,), jnp.bfloat16).at[targets]....]
  transfers between devices with their start and end apart: 13 -> 0, of which waited for: 6 -> 0; matrix products, arithmetic and copies ran while one was open for 20% -> 0% of each run, Pallas kernels for 0% -> 0%
where the time goes in v1:
time: 75.6 us; the launch traced here: 75.4 us
  Pallas kernels  72.3 us (96%)
  local copies, waits for them, and re-layouts  2.52 us (3%)
    pallas_call x1, Pallas kernels, dense_on_device(): pl.pallas_call(functools.partial(dense_kernel, cycle), out_shape=(jax.Sha...  72.3 us

profile of v1, /device:TPU:0, one launch (start us, length us, event | category | flops | bytes accessed | tf_op | source)
XLA Modules:
  0.0 75.4 jit_solution(7830653265447126349)
XLA Ops:
  0.6 72.3 %shard_map.50 = (f32[1,1024]{1,0:T(1,128)}, f32[2,1,256]{2,1,0:T(1,128)}) custom-call(s32[2,1,256]{2,1,0:T(1,128)} %bitcast.5, bf16[512,768]{1,0:T(8,128)(2,1)} %ingest_ref.1, bf16[1024,768]{1,0:T(8,128)(2,1)} %resident_ref.1), custom_call_target="tpu_custom_call" | custom-call | tf_op jit(solution)/shard_map/pallas_call | solution.py:366
  72.9 1.3 %log1p.12 = f32[1,1024]{1,0:T(1,128)} log-plus-one(f32[1,1024]{1,0:T(1,128)} %get-tuple-element.4) | non-fusion elementwise | bytes 8192 | tf_op jit(solution)/shard_map/log1p | solution.py:394
  74.2 1.2 %log1p.14 = f32[2,1,256]{2,1,0:T(1,128)} log-plus-one(f32[2,1,256]{2,1,0:T(1,128)} %get-tuple-element.5) | non-fusion elementwise | bytes 4096 | tf_op jit(solution)/shard_map/log1p | solution.py:394

commit v2 on v1

--- a/solution.py
+++ b/solution.py
@@ -109,13 +109,13 @@
 SUBLANES = 8
 INGEST_CHUNK = 256
 RESIDENT_CHUNK = 256
-TILE = 512
+TILE = 1024
 MESH = pl.DeviceIdType.MESH
 
 
 def dense_kernel(
     cycle, ids_ref, ingest_ref, resident_ref, resident_out, ingest_out,
-    rows, bank, ids, by_resident, by_ingest, resident_sums, ingest_sums, resident_terms, ingest_terms,
+    raw_ingest, raw_resident, load_sem, rows, bank, ids, by_resident, by_ingest, resident_sums, ingest_sums, resident_terms, ingest_terms,
     up_send, down_send, rows_recv, ids_send, ids_recv, peer_send, peer_recv, core_send, core_recv,
     relay_send, relay_recv, part_send, part_recv, term_send, term_recv,
 ):
@@ -197,15 +197,24 @@
             barrier, inc=1, device_id=device((line + hop) % line_size, side, core), device_id_type=MESH
         )
 
+    ingest_load = pltpu.make_async_copy(ingest_ref, raw_ingest, load_sem.at[0])
+    resident_load = pltpu.make_async_copy(resident_ref, raw_resident, load_sem.at[1])
+    ids_load = pltpu.make_async_copy(ids_ref, ids.at[pl.ds(line * chunks, chunks)], load_sem.at[2])
+    for load in (ingest_load, ids_load, resident_load):
+        load.start()
+
     def unit(block):
         values = block.astype(jnp.float32)
         squares = jnp.sum(values * values, axis=-1, keepdims=True) + epsilon
         return (values * lax.rsqrt(squares)).astype(jnp.bfloat16)
 
+    ingest_load.wait()
     for j in range(chunks):
-        rows[line * chunks + j] = unit(ingest_ref[j * INGEST_CHUNK:(j + 1) * INGEST_CHUNK, :])
-        ids[line * chunks + j] = ids_ref[j]
+        rows[line * chunks + j] = unit(raw_ingest[j * INGEST_CHUNK:(j + 1) * INGEST_CHUNK, :])
+    ids_load.wait()
     pl.semaphore_wait(barrier, line_size + 2)
+    for hop in range(1, line_size):
+        ids_copy((line + hop) % line_size).start()
     for j in range(chunks):
         @pl.when(line + 1 < line_size)
         def _():
@@ -214,21 +223,19 @@
         @pl.when(line > 0)
         def _():
             down_copy(line * chunks + j).start()
-    for hop in range(1, line_size):
-        ids_copy((line + hop) % line_size).start()
+
+    resident_load.wait()
 
     @pl.loop(0, pieces)
     def _(m):
         part = pl.ds(m * RESIDENT_CHUNK, RESIDENT_CHUNK)
-        bank[part, :] = unit(resident_ref[part, :])
+        bank[part, :] = unit(raw_resident[part, :])
 
     for m in range(pieces):
         peer_copy(m).start()
     core_copy.start()
     by_resident[...] = jnp.zeros_like(by_resident)
     by_ingest[...] = jnp.zeros_like(by_ingest)
-    for hop in range(1, line_size):
-        ids_arrival((line + hop) % line_size).wait_recv()
 
     scale = math.log2(math.e) / temper
     span = CL_OWN * cycle
@@ -261,6 +268,9 @@
         def _(j):
             work(line * chunks + j, half * tiles, (half + 1) * tiles)
 
+    for hop in range(1, line_size):
+        ids_arrival((line + hop) % line_size).wait_recv()
+
     @pl.loop(0, steps)
     def _(step):
         hop, j = step // chunks + 1, step % chunks
@@ -352,6 +362,11 @@
         other = (line + hop) % line_size
         ids_copy(other).wait_send()
         term_copy(other).wait_send()
+
+
+def score_kernel(resident_total, ingest_total, resident_score, ingest_score):
+    resident_score[...] = jnp.log1p(resident_total[...])
+    ingest_score[...] = jnp.log1p(ingest_total[...])
 
 
 def dense_on_device(cycle, resident, ingest, cluster_ids):
@@ -369,9 +384,12 @@
             jax.ShapeDtypeStruct((1, held), jnp.float32),
             jax.ShapeDtypeStruct((chunks, 1, INGEST_CHUNK), jnp.float32),
         ),
-        in_specs=[vmem] * 3,
+        in_specs=[pl.BlockSpec(memory_space=pl.ANY)] * 3,
         out_specs=(vmem, vmem),
         scratch_shapes=[
+            pltpu.VMEM((count, columns), jnp.bfloat16),
+            pltpu.VMEM((held, columns), jnp.bfloat16),
+            dma((3,)),
             pltpu.VMEM((blocks, INGEST_CHUNK, columns), jnp.bfloat16),
             pltpu.VMEM((4 * held, columns), jnp.bfloat16),
             pltpu.VMEM((blocks, 1, INGEST_CHUNK), jnp.int32),
@@ -391,7 +409,16 @@
         ],
         compiler_params=pltpu.CompilerParams(collective_id=0, has_side_effects=True),
     )(cluster_ids.reshape(chunks, 1, INGEST_CHUNK), ingest, resident)
-    return (jnp.log1p(resident_total.reshape(held)), jnp.log1p(ingest_total.reshape(count)))
+    resident_score, ingest_score = pl.pallas_call(
+        score_kernel,
+        out_shape=(
+            jax.ShapeDtypeStruct(resident_total.shape, jnp.float32),
+            jax.ShapeDtypeStruct(ingest_total.shape, jnp.float32),
+        ),
+        in_specs=[vmem] * 2,
+        out_specs=(vmem, vmem),
+    )(resident_total, ingest_total)
+    return (resident_score.reshape(held), ingest_score.reshape(count))
 
 
 def solution(mesh):

time: 75.6 us -> 66.8 us (0.88)
  Pallas kernels: 72.3 us -> 65.9 us
  local copies, waits for them, and re-layouts: 2.52 us -> 0 us
    pallas_call x1, Pallas kernels: 72.3 us -> 64.7 us  [dense_on_device(): pl.pallas_call(functools.partial(dense_kernel, cycle), out_shape=(jax.Sha...]
    log1p x2 -> x0, local copies, waits for them, and re-layouts: 2.52 us -> none  [the longest x1 1.28 us: dense_on_device(): jnp.log1p(resident_total.reshape(held))]
    pallas_call x0 -> x1, Pallas kernels: none -> 1.28 us  [dense_on_device(): pl.pallas_call(score_kernel, out_shape=(jax.ShapeDtypeStruct(resident_tot...]
where the time goes in v2:
time: 66.8 us; the launch traced here: 66.6 us
  Pallas kernels  65.9 us (99%)
    pallas_call x1, Pallas kernels, dense_on_device(): pl.pallas_call(functools.partial(dense_kernel, cycle), out_shape=(jax.Sha...  64.7 us

profile of v2, /device:TPU:0, one launch (start us, length us, event | category | flops | bytes accessed | tf_op | source)
XLA Modules:
  0.0 66.6 jit_solution(6371170995030899767)
XLA Ops:
  0.6 64.7 %shard_map.50 = (f32[1,1024]{1,0:T(1,128)}, f32[2,1,256]{2,1,0:T(1,128)}) custom-call(s32[2,1,256]{2,1,0:T(1,128)} %bitcast.3, bf16[512,768]{1,0:T(8,128)(2,1)} %ingest_ref.1, bf16[1024,768]{1,0:T(8,128)(2,1)} %resident_ref.1), custom_call_target="tpu_custom_call" | custom-call | tf_op jit(solution)/shard_map/pallas_call | solution.py:381
  65.3 1.3 %shard_map.51 = (f32[1,1024]{1,0:T(1,128)}, f32[2,1,256]{2,1,0:T(1,128)}) custom-call(f32[1,1024]{1,0:T(1,128)} %get-tuple-element.6.resident_total, f32[2,1,256]{2,1,0:T(1,128)} %get-tuple-element.7.ingest_total), custom_call_target="tpu_custom_call" | custom-call | tf_op jit(solution)/shard_map/pallas_call | solution.py:412

commit v3 on v2

--- a/solution.py
+++ b/solution.py
@@ -326,13 +326,15 @@
         block = by_resident[slot * held:(slot + 1) * held, :]
         resident_sums[slot] = jnp.sum(block.T, axis=0, keepdims=True)
 
-    for slot in (3, 2, 1):
-        gather_slot(slot)
+    gather_slot(3)
     for hop in range(1, line_size):
         term_copy((line + hop) % line_size).start()
+    gather_slot(2)
+    part_copy(3).start()
+    gather_slot(1)
+    part_copy(2).start()
     gather_slot(0)
-    for slot in (3, 2, 1):
-        part_copy(slot).start()
+    part_copy(1).start()
 
     for c in range(line_size * chunks):
         @pl.when((c // chunks <= line) & (line + 1 < line_size))

time: 66.8 us -> 66.5 us (level)
  no operation moved by 1% of the time
where the time goes in v3:
time: 66.5 us; the launch traced here: 66.3 us
  Pallas kernels  65.7 us (99%)
    pallas_call x1, Pallas kernels, dense_on_device(): pl.pallas_call(functools.partial(dense_kernel, cycle), out_shape=(jax.Sha...  64.4 us

profile of v3, /device:TPU:0, one launch (start us, length us, event | category | flops | bytes accessed | tf_op | source)
XLA Modules:
  0.0 66.3 jit_solution(12814455104187836392)
XLA Ops:
  0.6 64.4 %shard_map.50 = (f32[1,1024]{1,0:T(1,128)}, f32[2,1,256]{2,1,0:T(1,128)}) custom-call(s32[2,1,256]{2,1,0:T(1,128)} %bitcast.3, bf16[512,768]{1,0:T(8,128)(2,1)} %ingest_ref.1, bf16[1024,768]{1,0:T(8,128)(2,1)} %resident_ref.1), custom_call_target="tpu_custom_call" | custom-call | tf_op jit(solution)/shard_map/pallas_call | solution.py:383
  65.1 1.3 %shard_map.51 = (f32[1,1024]{1,0:T(1,128)}, f32[2,1,256]{2,1,0:T(1,128)}) custom-call(f32[1,1024]{1,0:T(1,128)} %get-tuple-element.6.resident_total, f32[2,1,256]{2,1,0:T(1,128)} %get-tuple-element.7.ingest_total), custom_call_target="tpu_custom_call" | custom-call | tf_op jit(solution)/shard_map/pallas_call | solution.py:414
